TPU v7x, 32 devices: a whole 2x2x4 slice. The times are simulated.
32 devices in a mesh: batch: 4 (over x, core), seq: 8 (over z, y).
Axes of the slice: x: 2, y: 2, z: 4, core: 2. Of those that a mesh axis runs over, the one named last changes fastest.
Arguments:
- layer_inputs: bfloat16 [25600, 800], P(('batch', 'seq')), may hold values from -24 to 24
- output_grads: bfloat16 [25600, 800], P(('batch', 'seq')), may hold values from -48 to 48
- input_inverse: float32 [800, 200], replicated, may hold values from -1 to 3
- output_inverse: float32 [800, 200], replicated, may hold values from -1 to 3
Outputs:
- input_factor: float32 [800, 200], P('seq')
- output_factor: float32 [800, 200], P('seq')
- preconditioned: bfloat16 [800, 800], replicated
All inputs are finite; a program needn't handle non-finite values.
Results may differ from a plain program's by a relative error of at most 0.0075.
Values may be sent and summed in bfloat16 or wider, within the bound.
A program may use at most 64 MiB of HBM per device.

v0:
```python
import functools

import jax
import jax.numpy as jnp
from jax import lax
from jax.experimental import pallas as pl
from jax.experimental.pallas import tpu as pltpu
from jax.sharding import PartitionSpec as P

BLOCK = 200


def block_terms(values):
    tok_rows, width = values.shape
    stacked = values.reshape(tok_rows, width // BLOCK, BLOCK)
    product = jnp.einsum("tnb,tnc->nbc", stacked, stacked, preferred_element_type=jnp.float32)
    return product.reshape(width, BLOCK)


def reduce_terms(input_term, output_term, grad_term):
    shares = (
        lax.psum_scatter(
            input_term.astype(jnp.bfloat16), "seq", scatter_dimension=0, tiled=True
        ).astype(jnp.float32),
        lax.psum_scatter(
            output_term.astype(jnp.bfloat16), "seq", scatter_dimension=0, tiled=True
        ).astype(jnp.float32),
        lax.psum_scatter(
            grad_term.astype(jnp.bfloat16), "seq", scatter_dimension=0, tiled=True
        ).astype(jnp.float32),
    )
    return lax.psum((shares[0], shares[1], shares[2]), "batch")


def shards(layer_inputs, output_grads, input_inverse, output_inverse):
    tok_rows, in_width = layer_inputs.shape
    out_width = output_grads.shape[1]
    in_blocks = in_width // BLOCK
    out_blocks = out_width // BLOCK
    total_rows = tok_rows * lax.axis_size("batch") * lax.axis_size("seq")
    inverse_count = 1.0 / total_rows
    input_term = block_terms(layer_inputs)
    output_term = block_terms(output_grads)
    input_stack = input_inverse.reshape(in_blocks, BLOCK, BLOCK)
    output_stack = output_inverse.reshape(out_blocks, BLOCK, BLOCK)
    grad_term = lax.dot_general(
        layer_inputs, output_grads, (((0,), (0,)), ((), ())), preferred_element_type=jnp.float32
    )
    input_sum, output_sum, grad_sum = reduce_terms(input_term, output_term, grad_term)
    grad_owned = grad_sum * inverse_count
    owned_rows = grad_owned.shape[0]
    right_done = jnp.einsum(
        "rmk,mkl->rml",
        grad_owned.reshape(owned_rows, out_blocks, BLOCK),
        output_stack,
        precision=lax.Precision.HIGHEST,
    ).reshape(owned_rows, out_width)
    gathered = lax.all_gather(right_done, "seq", axis=0, tiled=True)
    applied = jnp.einsum(
        "nij,njo->nio",
        input_stack,
        gathered.reshape(in_blocks, BLOCK, out_width),
        precision=lax.Precision.HIGHEST,
    ).reshape(in_width, out_width)
    preconditioned = applied.astype(jnp.bfloat16)
    input_factor = input_sum * inverse_count
    output_factor = output_sum * inverse_count
    return (input_factor, output_factor, preconditioned)


LANE = 128
PAD = 2 * LANE
MESH = pl.DeviceIdType.MESH


def round_up(size, unit):
    return (size + unit - 1) // unit * unit


def kernel(
    near, x_hbm, y_hbm, pinv_hbm, qinv_hbm, fx_ref, fy_ref, out_ref,
    x_ref, y_ref, pinv_ref, qinv_ref, load_s, xp, yp, g_own, g_away, g_stage, g_core, x_send, x_recv, y_send, y_recv, z_send, z_recv,
    f_own, f_stage, f_core, fy_send, fy_recv, fz_send, fz_recv, fx_send, fx_recv, fc_send, fc_recv,
    gc_send, gc_recv, ag,
    core_s, core_r, x_s, x_r, y_s, y_r, z_s, z_r, fy_s, fy_r, fz_s, fz_r, fin_s, fin_r,
    az_s, az_r, ay_s, ay_r, ax_s, ax_r, ac_s, ac_r,
):
    batch, seq = lax.axis_index("batch"), lax.axis_index("seq")
    x, c = batch // 2, batch % 2
    z, y = seq // 2, seq % 2
    tok, in_width = x_hbm.shape
    out_width = y_hbm.shape[1]
    in_blocks, out_blocks = in_width // BLOCK, out_width // BLOCK
    half_in = in_blocks // 2
    rows = g_own.shape[1]
    per_x = half_in * out_blocks
    window, step = f_own.shape[2], rows - f_own.shape[2]
    scale = 1.0 / (tok * lax.axis_size("batch") * lax.axis_size("seq"))
    core_peer = (2 * x + 1 - c, seq)
    x_peer = (2 * (1 - x) + c, seq)
    y_peer = (batch, 2 * z + 1 - y)

    def z_peer(to):
        return (batch, 2 * to + y)

    def around(i):
        return lax.rem(z + i, near)

    def remote(src, dst, s, r, peer):
        return pltpu.make_async_remote_copy(
            src_ref=src, dst_ref=dst, send_sem=s, recv_sem=r, device_id=peer, device_id_type=MESH
        )

    pending = []

    def send(*args):
        copy = remote(*args)
        copy.start()
        pending.append(copy)
        return copy

    loads = [
        pltpu.make_async_copy(src, dst, load_s.at[i])
        for i, (src, dst) in enumerate(
            ((x_hbm, x_ref), (y_hbm, y_ref), (pinv_hbm, pinv_ref), (qinv_hbm, qinv_ref))
        )
    ]
    for load in loads:
        load.start()
    barrier = pltpu.get_barrier_semaphore()
    peers = [core_peer, x_peer, y_peer] + [z_peer(around(i)) for i in range(1, near)]
    for peer in peers:
        pl.semaphore_signal(barrier, inc=1, device_id=peer, device_id_type=MESH)

    def padded(ref, out, blocks):
        for b in range(blocks):
            part = ref[:, b * BLOCK:(b + 1) * BLOCK]
            out[:, b * PAD:b * PAD + BLOCK] = part
            out[:, b * PAD + BLOCK:(b + 1) * PAD] = jnp.zeros((tok, PAD - BLOCK), out.dtype)

    loads[0].wait()
    padded(x_ref, xp, in_blocks)
    loads[1].wait()
    padded(y_ref, yp, out_blocks)

    def tdot(a, b):
        return lax.dot_general(a, b, (((0,), (0,)), ((), ())), preferred_element_type=jnp.float32)

    first = c == 0
    f32 = jnp.float32

    def mine(v):
        return jnp.where(first, v[:, :LANE], v[:, LANE:PAD])

    def other(v):
        return jnp.where(first, v[:, LANE:PAD], v[:, :LANE])

    far, own = 1 - z // 2, z // 2
    owners = out_blocks // 2

    def grads(to_x, keep, strip, base):
        col = pl.multiple_of((half_in * to_x + strip) * PAD, PAD)
        prod = tdot(xp[:, pl.ds(col, PAD)], yp[...])[:rows]
        for m in range(out_blocks):
            k = strip * out_blocks + m
            part = prod[:, m * PAD:(m + 1) * PAD]
            keep[k] = mine(part)
            g_stage[base + k] = other(part).astype(jnp.bfloat16)

    def swap(base, count, i):
        return send(g_stage.at[pl.ds(base, count)], g_core.at[pl.ds(base, count)], core_s.at[i], core_r.at[i], core_peer)

    grads(1 - x, g_away, far, 0)
    pl.semaphore_wait(barrier, len(peers))
    core_a = swap(far * out_blocks, out_blocks, 0)
    grads(1 - x, g_away, own, 0)
    core_b = swap(own * out_blocks, out_blocks, 1)

    def to_x(strip, core):
        core.wait_recv()
        for yy in (1 - y, y):
            for j in range(owners):
                k = 2 * (strip * owners + j) + yy
                x_send[k] = (g_away[k] + g_core[k].astype(f32)).astype(jnp.bfloat16)
                send(x_send.at[k], x_recv.at[k], x_s.at[k], x_r.at[k], x_peer)

    to_x(far, core_a)

    def factors(j, src):
        for b in range(in_blocks):
            part = src[:, b * PAD:(b + 1) * PAD]
            prod = tdot(part, part)
            keep, away = mine(prod), other(prod)
            for h in range(2):
                f_own[2 * b + h, j] = keep[h * step:h * step + window]
                f_stage[2 * b + h, j] = away[h * step:h * step + window].astype(jnp.bfloat16)

    factors(0, xp)
    to_x(own, core_b)
    factors(1, yp)
    core_f = send(f_stage, f_core, core_s.at[2], core_r.at[2], core_peer)
    for strip in (far, own):
        grads(x, g_own, strip, per_x)
    core_c = swap(per_x, per_x, 3)

    order = [far * owners + j for j in range(owners)]
    order += [own * owners + (z + 1 + j) % owners for j in range(owners)]

    def got_x(k):
        remote(x_send.at[k], x_recv.at[k], x_s.at[k], x_r.at[k], x_peer).wait_recv()
        return g_own[k] + g_core[per_x + k].astype(f32) + x_recv[k].astype(f32)

    def grad_y(to):
        y_send[to] = got_x(2 * to + 1 - y).astype(jnp.bfloat16)
        send(y_send.at[to], y_recv.at[to], y_s.at[to], y_r.at[to], y_peer)

    def factor_y(to):
        k = 2 * to + 1 - y
        fy_send[to] = (f_own[k] + f_core[k].astype(f32)).astype(jnp.bfloat16)
        send(fy_send.at[to], fy_recv.at[to], fy_s.at[to], fy_r.at[to], y_peer)

    def got_factor(to):
        k = 2 * to + y
        remote(fy_send.at[to], fy_recv.at[to], fy_s.at[to], fy_r.at[to], y_peer).wait_recv()
        return f_own[k] + f_core[k].astype(f32) + fy_recv[to].astype(f32)

    def factor_z(to):
        fz_send[to] = got_factor(to).astype(jnp.bfloat16)
        send(fz_send.at[to], fz_recv.at[z], fz_s.at[to], fz_r.at[z], z_peer(to))

    def got_grad(to):
        t = got_x(2 * to + y)
        remote(y_send.at[to], y_recv.at[to], y_s.at[to], y_r.at[to], y_peer).wait_recv()
        return t + y_recv[to].astype(f32)

    def grad_z(to):
        z_send[to] = got_grad(to).astype(jnp.bfloat16)
        send(z_send.at[to], z_recv.at[z], z_s.at[to], z_r.at[z], z_peer(to))

    core_f.wait_recv()
    early = order[:owners]
    for to in early:
        factor_y(to)
    core_c.wait_recv()
    for to in early:
        grad_y(to)
    for to in early:
        factor_z(to)
    late = order[owners:]
    for to in late:
        grad_y(to)
    for to in late:
        factor_y(to)
    for to in early:
        grad_z(to)
    for to in late[:-1]:
        grad_z(to)
    gc_send[...] = got_grad(z)
    for to in late[:-1]:
        factor_z(to)
    f_total = got_factor(z)

    def z_sum(sends, recvs, s, r, total):
        for src in order[:-1]:
            remote(sends.at[src], recvs.at[src], s.at[src], r.at[src], z_peer(src)).wait_recv()
            total = total + recvs[src].astype(f32)
        return total

    block = x * per_x + seq
    b, m = block // out_blocks, block % out_blocks
    loads[2].wait()
    loads[3].wait()

    def pick(ref, which, count):
        part = ref[:, :BLOCK]
        for n in range(1, count):
            part = jnp.where(which == n, ref[:, n * BLOCK:(n + 1) * BLOCK], part)
        return part

    p_t = pick(pinv_ref, b, in_blocks)
    q_t = pick(qinv_ref, m, out_blocks)
    q_tail = jnp.concatenate([q_t[LANE:], jnp.zeros((PAD - BLOCK, BLOCK), f32)], axis=0)
    q_half = jnp.where(first, q_t[:LANE], q_tail)
    p_now = p_t.T

    gc_send[...] = z_sum(z_send, z_recv, z_s, z_r, gc_send[...])
    fin_g = send(gc_send, gc_recv, fin_s.at[1], fin_r.at[1], core_peer)
    fin_g.wait_recv()
    ours, theirs = gc_send[...], gc_recv[...]
    left = jnp.where(first, ours, theirs)[:BLOCK]
    right = jnp.where(first, theirs, ours)[:BLOCK]
    full = jnp.concatenate([left, right[:, :BLOCK - LANE]], axis=1) * scale
    right_done = lax.dot_general(
        full, q_half, (((1,), (1,)), ((), ())), precision=lax.Precision.HIGHEST, preferred_element_type=f32
    )
    applied = jnp.dot(p_now, right_done, precision=lax.Precision.HIGHEST, preferred_element_type=f32)
    applied = jnp.concatenate([applied, jnp.zeros((rows - BLOCK, LANE), f32)], axis=0)
    ag[c, block] = applied.astype(jnp.bfloat16)

    def gather(g, s, r, peer):
        return remote(ag.at[c, g], ag.at[c, g], s, r, peer)

    def start(copy):
        copy.start()
        pending.append(copy)

    base, away = x * per_x, (1 - x) * per_x
    for to in order[:-1]:
        start(gather(block, az_s.at[to], az_r.at[z], z_peer(to)))

    def on_y(g, slot):
        start(gather(g, ay_s.at[slot], ay_r.at[slot], y_peer))

    def on_x(k):
        start(gather(base + k, ax_s.at[k], ax_r.at[k], x_peer))

    def on_core(g):
        start(gather(g, ac_s.at[g], ac_r.at[g], core_peer))

    def arrived_y(i):
        zz = around(i)
        k = 2 * zz + 1 - y
        gather(base + k, ay_s.at[zz], ay_r.at[zz], y_peer).wait_recv()
        on_x(k)
        on_core(base + k)

    def arrived_x(i):
        zz = around(i)
        k = 2 * zz + y
        gather(away + k, ax_s.at[k], ax_r.at[k], x_peer).wait_recv()
        on_core(away + k)

    def arrived_far(i):
        zz = around(i)
        k = 2 * zz + 1 - y
        gather(away + k, ax_s.at[k], ax_r.at[k], x_peer).wait_recv()
        on_core(away + k)

    on_x(seq)
    on_y(block, z)
    on_core(block)

    f_total = z_sum(fz_send, fz_recv, fz_s, fz_r, f_total)
    fx_send[...] = f_total.astype(jnp.bfloat16)
    fin_x = send(fx_send, fx_recv, fin_s.at[0], fin_r.at[0], x_peer)

    for i in range(1, near):
        src = around(i)
        k = 2 * src + y
        gather(base + k, az_s.at[src], az_r.at[src], z_peer(src)).wait_recv()
        on_y(base + k, src)
        on_x(k)
        on_core(base + k)
        arrived_y(i - 1)
        arrived_x(i - 1)

    fin_x.wait_recv()
    fc_send[...] = fx_send[...].astype(f32) + fx_recv[...].astype(f32)
    fin_c = send(fc_send, fc_recv, fin_s.at[2], fin_r.at[2], core_peer)
    arrived_y(near - 1)
    arrived_x(near - 1)

    fin_c.wait_recv()
    take = fx_ref.shape[1]
    skip = take - step
    for j, ref in enumerate((fx_ref, fy_ref)):
        ours, theirs = fc_send[j], fc_recv[j]
        left = jnp.where(first, ours, theirs)
        right = jnp.where(first, theirs, ours)
        both = jnp.concatenate([left, right[:, :BLOCK - LANE]], axis=1) * scale
        ref[...] = jnp.where(y == 0, both[:take], both[skip:skip + take]).T

    for i in range(near):
        arrived_far(i)
    for g in range(2 * per_x):
        remote(ag.at[1 - c, g], ag.at[1 - c, g], ac_s.at[g], ac_r.at[g], core_peer).wait_recv()

    for pair in range(in_blocks // 2):
        strips = []
        for bi in (2 * pair, 2 * pair + 1):
            parts = []
            for mi in range(out_blocks):
                g = bi * out_blocks + mi
                parts.append(ag[0, g].astype(f32)[:BLOCK])
                parts.append(ag[1, g].astype(f32)[:BLOCK, :BLOCK - LANE])
            strips.append(jnp.concatenate(parts, axis=1))
        whole = jnp.concatenate(strips, axis=0).astype(jnp.bfloat16)
        out_ref[2 * pair * BLOCK:2 * (pair + 1) * BLOCK, :] = whole
    for copy in pending:
        copy.wait_send()


def fused(layer_inputs, output_grads, input_inverse, output_inverse):
    tok, in_width = layer_inputs.shape
    out_width = output_grads.shape[1]
    in_blocks, out_blocks = in_width // BLOCK, out_width // BLOCK
    seq = lax.axis_size("seq")
    near = seq // 2
    rows = round_up(BLOCK, 16)
    take = in_width // seq
    step = take // 16 * 16
    window = rows - step
    blocks = in_blocks * out_blocks
    per_x = blocks // 2
    bf16, f32 = jnp.bfloat16, jnp.float32
    vmem = pltpu.VMEM
    dma = pltpu.SemaphoreType.DMA
    g = (rows, LANE)
    f = (2, window, LANE)
    hbm = pl.BlockSpec(memory_space=pltpu.HBM)
    scratch = [
        vmem(layer_inputs.shape, bf16),
        vmem(output_grads.shape, bf16),
        vmem((BLOCK, in_width), f32),
        vmem((BLOCK, out_width), f32),
        dma((4,)),
        vmem((tok, in_blocks * PAD), bf16),
        vmem((tok, out_blocks * PAD), bf16),
        vmem((per_x, *g), f32),
        vmem((per_x, *g), f32),
        vmem((blocks, *g), bf16),
        vmem((blocks, *g), bf16),
        vmem((per_x, *g), bf16),
        vmem((per_x, *g), bf16),
        vmem((near, *g), bf16),
        vmem((near, *g), bf16),
        vmem((near, *g), bf16),
        vmem((near, *g), bf16),
        vmem((seq, *f), f32),
        vmem((seq, *f), bf16),
        vmem((seq, *f), bf16),
        vmem((near, *f), bf16),
        vmem((near, *f), bf16),
        vmem((near, *f), bf16),
        vmem((near, *f), bf16),
        vmem(f, bf16),
        vmem(f, bf16),
        vmem(f, f32),
        vmem(f, f32),
        vmem(g, f32),
        vmem(g, f32),
        vmem((2, blocks, *g), bf16),
    ]
    for count in (4, per_x, near, near, near, near, 3, near, 2 * near, per_x, blocks):
        scratch += [dma((count,)), dma((count,))]
    fx, fy, out = pl.pallas_call(
        functools.partial(kernel, near),
        out_shape=(
            jax.ShapeDtypeStruct((BLOCK, take), f32),
            jax.ShapeDtypeStruct((BLOCK, out_width // seq), f32),
            jax.ShapeDtypeStruct((in_width, out_width), bf16),
        ),
        in_specs=[hbm] * 4,
        out_specs=(pl.BlockSpec(memory_space=vmem),) * 3,
        scratch_shapes=scratch,
        compiler_params=pltpu.CompilerParams(
            collective_id=0, has_side_effects=True, vmem_limit_bytes=67043328
        ),
    )(layer_inputs, output_grads, input_inverse.T, output_inverse.T)
    return fx.T, fy.T, out


def solution(mesh):
    def step(layer_inputs, output_grads, input_inverse, output_inverse):
        in_width, out_width = layer_inputs.shape[1], output_grads.shape[1]
        in_blocks, out_blocks = in_width // BLOCK, out_width // BLOCK
        fits = (
            mesh.shape["batch"] == 4
            and in_blocks * out_blocks == 2 * mesh.shape["seq"]
            and in_blocks == out_blocks
            and 2 * in_blocks == mesh.shape["seq"]
            and in_blocks // 2 == 2
        )
        body = fused if fits else shards
        return body(layer_inputs, output_grads, input_inverse, output_inverse)

    return jax.shard_map(
        step,
        mesh=mesh,
        in_specs=(P(("batch", "seq"), None), P(("batch", "seq"), None), P(), P()),
        out_specs=(P("seq", None), P("seq", None), P()),
        check_vma=False,
    )
```

profile of v0, /device:TPU:0, one launch (start us, length us, event | category | flops | bytes accessed | tf_op | source)
XLA Modules:
  0.0 51.2 jit_solution(2039012958808504423)
XLA Ops:
  0.6 44.9 %shard_map.67 = (f32[200,100]{1,0:T(8,128)}, f32[200,100]{1,0:T(8,128)}, bf16[800,800]{1,0:T(8,128)(2,1)}) custom-call(bf16[800,800]{1,0:T(8,128)(2,1)} %x_hbm.1, bf16[800,800]{1,0:T(8,128)(2,1)} %y_hbm.1, f32[200,800]{1,0:T(8,128)} %bitcast.4, f32[200,800]{1,0:T(8,128)} %bitcast.5), custom_call_target="tpu_custom_call" | custom-call | tf_op jit(solution)/shard_map/pallas_call | solution.py:446
  45.5 1.5 %copy.10 = f32[100,200]{0,1:T(8,128)} copy(f32[100,200]{0,1:T(8,128)} %bitcast.7) | data formatting | bytes 160000
  47.1 1.5 %copy.11 = f32[100,200]{0,1:T(8,128)} copy(f32[100,200]{0,1:T(8,128)} %bitcast.6) | data formatting | bytes 160000
  48.6 2.6 %copy.12 = bf16[800,800]{1,0:T(8,128)(2,1)} copy(bf16[800,800]{1,0:T(8,128)(2,1)} %get-tuple-element.14) | data formatting | bytes 2560000
where the time goes:
time: 51.8 us; the launch traced here: 51.2 us
  Pallas kernels  44.9 us (87%)
  local copies, waits for them, and re-layouts  5.65 us (11%)
  between operations  0.64 us (1%)
    pallas_call x1, Pallas kernels, fused(): pl.pallas_call(functools.partial(kernel, near), out_shape=(jax.ShapeDtype...  44.9 us
    unnamed x3, local copies, waits for them, and re-layouts  5.65 us

commit v1 on v0

--- a/solution.py
+++ b/solution.py
@@ -446,18 +446,41 @@
     fx, fy, out = pl.pallas_call(
         functools.partial(kernel, near),
         out_shape=(
-            jax.ShapeDtypeStruct((BLOCK, take), f32),
-            jax.ShapeDtypeStruct((BLOCK, out_width // seq), f32),
-            jax.ShapeDtypeStruct((in_width, out_width), bf16),
+            pltpu.VMEM((BLOCK, take), f32),
+            pltpu.VMEM((BLOCK, out_width // seq), f32),
+            pltpu.VMEM((in_width, out_width), bf16),
         ),
         in_specs=[hbm] * 4,
         out_specs=(pl.BlockSpec(memory_space=vmem),) * 3,
         scratch_shapes=scratch,
         compiler_params=pltpu.CompilerParams(
-            collective_id=0, has_side_effects=True, vmem_limit_bytes=67043328
+            collective_id=0, has_side_effects=True, vmem_limit_bytes=62000000
         ),
     )(layer_inputs, output_grads, input_inverse.T, output_inverse.T)
+    fx, fy, out = settle(fx, fy, out)
     return fx.T, fy.T, out
+
+
+def settle_kernel(a, b, c, a_out, b_out, c_out, sems):
+    copies = [
+        pltpu.make_async_copy(src, dst, sems.at[i])
+        for i, (src, dst) in enumerate(((a, a_out), (b, b_out), (c, c_out)))
+    ]
+    for copy in copies:
+        copy.start()
+    for copy in copies:
+        copy.wait()
+
+
+def settle(*arrays):
+    return pl.pallas_call(
+        settle_kernel,
+        out_shape=tuple(jax.ShapeDtypeStruct(a.shape, a.dtype) for a in arrays),
+        in_specs=[pl.BlockSpec(memory_space=pltpu.VMEM)] * 3,
+        out_specs=(pl.BlockSpec(memory_space=pltpu.HBM),) * 3,
+        scratch_shapes=[pltpu.SemaphoreType.DMA((3,))],
+        compiler_params=pltpu.CompilerParams(vmem_limit_bytes=4 * 2**20),
+    )(*arrays)
 
 
 def solution(mesh):

time: 51.8 us -> 46.1 us (0.89)
  local copies, waits for them, and re-layouts: 5.65 us -> 0 us
    unnamed x3 -> x0, local copies, waits for them, and re-layouts: 5.65 us -> none
    pallas_call x1 -> x2, Pallas kernels: 44.9 us -> 44.9 us  [the longest x1 43.7 us: fused(): pl.pallas_call(functools.partial(kernel, near), out_shape=(pltpu.VMEM((BL...]
where the time goes in v1:
time: 46.1 us; the launch traced here: 45.5 us
  Pallas kernels  44.9 us (97%)
  between operations  0.64 us (1%)
    pallas_call x1, Pallas kernels, fused(): pl.pallas_call(functools.partial(kernel, near), out_shape=(pltpu.VMEM((BL...  43.7 us
    pallas_call x1, Pallas kernels, settle(): pl.pallas_call(settle_kernel, out_shape=tuple((jax.ShapeDtypeStruct(a.sha...  1.19 us

profile of v1, /device:TPU:0, one launch (start us, length us, event | category | flops | bytes accessed | tf_op | source)
XLA Modules:
  0.0 45.5 jit_solution(15915866117825696843)
XLA Ops:
  0.6 43.7 %shard_map.67 = (f32[200,100]{1,0:T(8,128)S(1)}, f32[200,100]{1,0:T(8,128)S(1)}, bf16[800,800]{1,0:T(8,128)(2,1)S(1)}) custom-call(bf16[800,800]{1,0:T(8,128)(2,1)} %x_hbm.1, bf16[800,800]{1,0:T(8,128)(2,1)} %y_hbm.1, f32[200,800]{1,0:T(8,128)} %bitcast.4, f32[200,800]{1,0:T(8,128)} %bitcast.5), custom_call_target="tpu_custom_call" | custom-call | tf_op jit(solution)/shard_map/pallas_call | solution.py:446
  44.3 1.2 %shard_map.68 = (f32[200,100]{1,0:T(8,128)}, f32[200,100]{1,0:T(8,128)}, bf16[800,800]{1,0:T(8,128)(2,1)}) custom-call(f32[200,100]{1,0:T(8,128)S(1)} %get-tuple-element.9.a, f32[200,100]{1,0:T(8,128)S(1)} %get-tuple-element.10.b, bf16[800,800]{1,0:T(8,128)(2,1)S(1)} %get-tuple-element.11.c), custom_call_target="tpu_custom_call" | custom-call | tf_op jit(solution)/shard_map/pallas_call | solution.py:476

commit v2 on v1

v2 whole, which is shorter than its diff:
```python
import functools

import jax
import jax.numpy as jnp
from jax import lax
from jax.experimental import pallas as pl
from jax.experimental.pallas import tpu as pltpu
from jax.sharding import PartitionSpec as P

BLOCK = 200


def block_terms(values):
    tok_rows, width = values.shape
    stacked = values.reshape(tok_rows, width // BLOCK, BLOCK)
    product = jnp.einsum("tnb,tnc->nbc", stacked, stacked, preferred_element_type=jnp.float32)
    return product.reshape(width, BLOCK)


def reduce_terms(input_term, output_term, grad_term):
    shares = (
        lax.psum_scatter(
            input_term.astype(jnp.bfloat16), "seq", scatter_dimension=0, tiled=True
        ).astype(jnp.float32),
        lax.psum_scatter(
            output_term.astype(jnp.bfloat16), "seq", scatter_dimension=0, tiled=True
        ).astype(jnp.float32),
        lax.psum_scatter(
            grad_term.astype(jnp.bfloat16), "seq", scatter_dimension=0, tiled=True
        ).astype(jnp.float32),
    )
    return lax.psum((shares[0], shares[1], shares[2]), "batch")


def shards(layer_inputs, output_grads, input_inverse, output_inverse):
    tok_rows, in_width = layer_inputs.shape
    out_width = output_grads.shape[1]
    in_blocks = in_width // BLOCK
    out_blocks = out_width // BLOCK
    total_rows = tok_rows * lax.axis_size("batch") * lax.axis_size("seq")
    inverse_count = 1.0 / total_rows
    input_term = block_terms(layer_inputs)
    output_term = block_terms(output_grads)
    input_stack = input_inverse.reshape(in_blocks, BLOCK, BLOCK)
    output_stack = output_inverse.reshape(out_blocks, BLOCK, BLOCK)
    grad_term = lax.dot_general(
        layer_inputs, output_grads, (((0,), (0,)), ((), ())), preferred_element_type=jnp.float32
    )
    input_sum, output_sum, grad_sum = reduce_terms(input_term, output_term, grad_term)
    grad_owned = grad_sum * inverse_count
    owned_rows = grad_owned.shape[0]
    right_done = jnp.einsum(
        "rmk,mkl->rml",
        grad_owned.reshape(owned_rows, out_blocks, BLOCK),
        output_stack,
        precision=lax.Precision.HIGHEST,
    ).reshape(owned_rows, out_width)
    gathered = lax.all_gather(right_done, "seq", axis=0, tiled=True)
    applied = jnp.einsum(
        "nij,njo->nio",
        input_stack,
        gathered.reshape(in_blocks, BLOCK, out_width),
        precision=lax.Precision.HIGHEST,
    ).reshape(in_width, out_width)
    preconditioned = applied.astype(jnp.bfloat16)
    input_factor = input_sum * inverse_count
    output_factor = output_sum * inverse_count
    return (input_factor, output_factor, preconditioned)


LANE = 128
PAD = 2 * LANE
MESH = pl.DeviceIdType.MESH


def round_up(size, unit):
    return (size + unit - 1) // unit * unit


def kernel(
    near, x_hbm, y_hbm, pinv_hbm, qinv_hbm, fx_ref, fy_ref, out_ref,
    x_ref, y_ref, pinv_ref, qinv_ref, load_s, xp, yp, xq, yq, own, stage, core,
    x_send, x_recv, y_send, y_recv, z_send, z_recv,
    f_own, f_stage, f_core, fy_send, fy_recv, fz_send, fz_recv, fx_send, fx_recv, fc_send, fc_recv, ag,
    core_s, core_r, x_s, x_r, y_s, y_r, z_s, z_r, fy_s, fy_r, fz_s, fz_r, fin_s, fin_r,
    az_s, az_r, ay_s, ay_r, ax_s, ax_r, ac_s, ac_r,
):
    batch, seq = lax.axis_index("batch"), lax.axis_index("seq")
    x, c = batch // 2, batch % 2
    z, y = seq // 2, seq % 2
    tok, in_width = x_hbm.shape
    out_width = y_hbm.shape[1]
    in_blocks, out_blocks = in_width // BLOCK, out_width // BLOCK
    strip = own.shape[2]
    tiles = near - 1
    whole = 2 * tiles * LANE
    rest = out_width - whole
    mid = in_width // strip // 2
    window, step = f_own.shape[2], round_up(BLOCK, 16) - f_own.shape[2]
    scale = 1.0 / (tok * lax.axis_size("batch") * lax.axis_size("seq"))
    core_peer = (2 * x + 1 - c, seq)
    x_peer = (2 * (1 - x) + c, seq)
    y_peer = (batch, 2 * z + 1 - y)
    f32, bf16 = jnp.float32, jnp.bfloat16
    first = c == 0

    def z_peer(to):
        return (batch, 2 * to + y)

    by_distance = [z + 1 - 2 * (z % 2), 2 - z // 2, 3 * (1 - z // 2)]
    others = by_distance[::-1]

    def remote(src, dst, s, r, peer):
        return pltpu.make_async_remote_copy(
            src_ref=src, dst_ref=dst, send_sem=s, recv_sem=r, device_id=peer, device_id_type=MESH
        )

    pending = []

    def send(*args):
        copy = remote(*args)
        copy.start()
        pending.append(copy)
        return copy

    loads = [
        pltpu.make_async_copy(src, dst, load_s.at[i])
        for i, (src, dst) in enumerate(
            ((x_hbm, x_ref), (pinv_hbm, pinv_ref), (y_hbm, y_ref), (qinv_hbm, qinv_ref))
        )
    ]
    for load in loads:
        load.start()
    barrier = pltpu.get_barrier_semaphore()
    peers = [core_peer, x_peer, y_peer] + [z_peer(to) for to in others]
    for peer in peers:
        pl.semaphore_signal(barrier, inc=1, device_id=peer, device_id_type=MESH)

    def padded(ref, out, blocks):
        for b in range(blocks):
            part = ref[:, b * BLOCK:(b + 1) * BLOCK]
            out[:, b * PAD:b * PAD + BLOCK] = part
            out[:, b * PAD + BLOCK:(b + 1) * PAD] = jnp.zeros((tok, PAD - BLOCK), out.dtype)

    def two_terms(v):
        high = v.astype(bf16)
        low = (v - high.astype(f32)).astype(bf16)
        return jnp.concatenate([high, low], axis=1)

    def last_dims(a, b):
        return lax.dot_general(a, b, (((1,), (1,)), ((), ())), preferred_element_type=f32)

    def tdot(a, b):
        return lax.dot_general(a, b, (((0,), (0,)), ((), ())), preferred_element_type=f32)

    def twice(v):
        return jnp.concatenate([v, v], axis=1)

    fill = PAD - BLOCK
    loads[0].wait()
    padded(x_ref, xp, in_blocks)
    loads[1].wait()
    for b in range(in_blocks):
        p_t = pinv_ref[:, b * BLOCK:(b + 1) * BLOCK]
        p = jnp.concatenate([p_t, jnp.zeros((fill, BLOCK), f32)], axis=0).T
        part = last_dims(two_terms(p), twice(xp[:, b * PAD:(b + 1) * PAD]))
        xq[b * BLOCK:(b + 1) * BLOCK, :] = part.astype(bf16)
    loads[2].wait()
    padded(y_ref, yp, out_blocks)
    loads[3].wait()
    for m in range(out_blocks):
        q_t = qinv_ref[:, m * BLOCK:(m + 1) * BLOCK]
        q_t = jnp.concatenate([q_t, jnp.zeros((BLOCK, fill), f32)], axis=1)
        part = last_dims(twice(yp[:, m * PAD:(m + 1) * PAD]), two_terms(q_t))
        yq[:, m * BLOCK:(m + 1) * BLOCK] = part.astype(bf16)
    yq[:, out_width:] = jnp.zeros((tok, yq.shape[1] - out_width), bf16)

    def keep(group, k, left, right):
        own[group, k] = jnp.where(first, left, right)
        stage[group, k] = jnp.where(first, right, left).astype(bf16)

    def product(row):
        rows = pl.ds(pl.multiple_of(strip * row, strip), strip)
        return jnp.dot(xq[rows, :], yq[:, :whole], preferred_element_type=f32)

    def tile(v, t):
        return v[:, t * LANE:(t + 1) * LANE]

    def strips(to_x, to_y):
        row = to_x * (2 * mid - 2 * to_y) + to_y
        v = product(row)
        for t in range(tiles):
            keep(2 * to_x + to_y, t, tile(v, t), tile(v, tiles + t))

    def middle():
        v = product(mid)
        for t in range(tiles):
            keep(t, tiles, tile(v, t), tile(v, tiles + t))
        tail = jnp.dot(xq[...], yq[:, whole:], preferred_element_type=f32)
        folded = tail[:BLOCK]
        for b in range(1, in_blocks):
            folded = folded + pltpu.roll(tail[b * BLOCK:(b + 1) * BLOCK], b * rest, 1)
        skip = BLOCK // 16 * 8
        take = BLOCK - skip
        none = jnp.zeros((strip - take, LANE), f32)
        keep(tiles, tiles, jnp.concatenate([folded[:take], none], axis=0), jnp.concatenate([folded[skip:], none], axis=0))

    def swap(at, i):
        return send(stage.at[at], core.at[at], core_s.at[i], core_r.at[i], core_peer)

    far_far, far_own = 2 * (1 - x) + 1 - y, 2 * (1 - x) + y
    strips(1 - x, 1 - y)
    pl.semaphore_wait(barrier, len(peers))
    core_a = swap((far_far, pl.ds(0, tiles)), 0)
    strips(1 - x, y)
    core_b = swap((far_own, pl.ds(0, tiles)), 1)

    def on_chip(group, k):
        return own[group, k] + core[group, k].astype(f32)

    def to_x(yy, k):
        x_send[yy, k] = on_chip(2 * (1 - x) + yy, k).astype(bf16)
        i = near * yy + k
        send(x_send.at[yy, k], x_recv.at[yy, k], x_s.at[i], x_r.at[i], x_peer)

    core_a.wait_recv()
    for k in range(tiles):
        to_x(1 - y, k)
    middle()
    core_c = swap((pl.ds(0, 4), tiles), 2)
    core_b.wait_recv()
    core_c.wait_recv()
    to_x(1 - y, tiles)
    for k in others + [z]:
        to_x(y, k)

    def mine(v):
        return jnp.where(first, v[:, :LANE], v[:, LANE:PAD])

    def other(v):
        return jnp.where(first, v[:, LANE:PAD], v[:, :LANE])

    def factors(j, src):
        for b in range(in_blocks):
            part = src[:, b * PAD:(b + 1) * PAD]
            prod = tdot(part, part)
            kept, away = mine(prod), other(prod)
            for h in range(2):
                f_own[2 * b + h, j] = kept[h * step:h * step + window]
                f_stage[2 * b + h, j] = away[h * step:h * step + window].astype(bf16)

    factors(0, xp)
    factors(1, yp)
    core_f = send(f_stage, f_core, core_s.at[3], core_r.at[3], core_peer)
    strips(x, 1 - y)
    strips(x, y)
    core_d = swap((pl.ds(2 * x, 2), pl.ds(0, tiles)), 4)

    def got_x(yy, k):
        i = near * yy + k
        remote(x_send.at[yy, k], x_recv.at[yy, k], x_s.at[i], x_r.at[i], x_peer).wait_recv()
        return on_chip(2 * x + yy, k) + x_recv[yy, k].astype(f32)

    def grad_y(to):
        y_send[to] = got_x(1 - y, to).astype(bf16)
        send(y_send.at[to], y_recv.at[to], y_s.at[to], y_r.at[to], y_peer)

    def factor_y(to):
        k = 2 * to + 1 - y
        fy_send[to] = (f_own[k] + f_core[k].astype(f32)).astype(bf16)
        send(fy_send.at[to], fy_recv.at[to], fy_s.at[to], fy_r.at[to], y_peer)

    def got_factor(to):
        k = 2 * to + y
        remote(fy_send.at[to], fy_recv.at[to], fy_s.at[to], fy_r.at[to], y_peer).wait_recv()
        return f_own[k] + f_core[k].astype(f32) + fy_recv[to].astype(f32)

    def factor_z(to):
        fz_send[to] = got_factor(to).astype(bf16)
        send(fz_send.at[to], fz_recv.at[z], fz_s.at[to], fz_r.at[z], z_peer(to))

    def got_grad(to):
        total = got_x(y, to)
        remote(y_send.at[to], y_recv.at[to], y_s.at[to], y_r.at[to], y_peer).wait_recv()
        return total + y_recv[to].astype(f32)

    def grad_z(to):
        z_send[to] = got_grad(to).astype(bf16)
        send(z_send.at[to], z_recv.at[z], z_s.at[to], z_r.at[z], z_peer(to))

    core_f.wait_recv()
    for to in others[:2]:
        factor_y(to)
    core_d.wait_recv()
    grad_y(0)
    grad_y(1)
    for to in others[:2]:
        factor_z(to)
    grad_y(2)
    factor_y(others[2])
    grad_y(3)
    factor_y(z)
    for to in others:
        grad_z(to)
    factor_z(others[2])
    g_total = got_grad(z)
    f_total = got_factor(z)

    def z_sum(sends, recvs, s, r, total):
        for src in by_distance:
            remote(sends.at[src], recvs.at[src], s.at[src], r.at[src], z_peer(src)).wait_recv()
            total = total + recvs[src].astype(f32)
        return total

    here = 2 * x + y
    ag[c, here, z] = (z_sum(z_send, z_recv, z_s, z_r, g_total) * scale).astype(bf16)

    def gather(group, k, s, r, peer):
        return remote(ag.at[c, group, k], ag.at[c, group, k], s, r, peer)

    def start(copy):
        copy.start()
        pending.append(copy)

    by_x, by_y, across = 2 * (1 - x) + y, 2 * x + 1 - y, 2 * (1 - x) + 1 - y

    def on_core(group, k):
        i = near * group + k
        start(gather(group, k, ac_s.at[i], ac_r.at[i], core_peer))

    def spread(k):
        start(gather(here, k, ay_s.at[k], ay_r.at[k], y_peer))
        start(gather(here, k, ax_s.at[k], ax_r.at[k], x_peer))
        on_core(here, k)

    def arrived_z(src):
        gather(here, src, az_s.at[src], az_r.at[src], z_peer(src)).wait_recv()
        spread(src)

    def arrived_x(k, forward):
        gather(by_x, k, ax_s.at[k], ax_r.at[k], x_peer).wait_recv()
        if forward:
            start(gather(by_x, k, ay_s.at[near + k], ay_r.at[near + k], y_peer))
        on_core(by_x, k)

    def arrived_y(k, forward):
        gather(by_y, k, ay_s.at[k], ay_r.at[k], y_peer).wait_recv()
        if forward:
            start(gather(by_y, k, ax_s.at[near + k], ax_r.at[near + k], x_peer))
        on_core(by_y, k)

    def arrived_across(k, on_y):
        if on_y:
            gather(across, k, ay_s.at[near + k], ay_r.at[near + k], y_peer).wait_recv()
        else:
            gather(across, k, ax_s.at[near + k], ax_r.at[near + k], x_peer).wait_recv()
        on_core(across, k)

    for to in others:
        start(gather(here, z, az_s.at[to], az_r.at[z], z_peer(to)))
    spread(z)

    f_total = z_sum(fz_send, fz_recv, fz_s, fz_r, f_total)
    fx_send[...] = f_total.astype(bf16)
    fin_x = send(fx_send, fx_recv, fin_s.at[0], fin_r.at[0], x_peer)

    arrival = [z] + by_distance
    for i in range(1, near):
        arrived_z(arrival[i])
        arrived_x(arrival[i - 1], i % 2 == 1)
        arrived_y(arrival[i - 1], i % 2 == 0)
    fin_x.wait_recv()
    fc_send[...] = fx_send[...].astype(f32) + fx_recv[...].astype(f32)
    fin_c = send(fc_send, fc_recv, fin_s.at[1], fin_r.at[1], core_peer)
    arrived_x(arrival[-1], False)
    arrived_y(arrival[-1], True)
    for i in range(near):
        arrived_across(arrival[i], i % 2 == 0)

    fin_c.wait_recv()
    take = fx_ref.shape[1]
    skip = take - step
    for j, ref in enumerate((fx_ref, fy_ref)):
        ours, theirs = fc_send[j], fc_recv[j]
        left = jnp.where(first, ours, theirs)
        right = jnp.where(first, theirs, ours)
        both = jnp.concatenate([left, right[:, :BLOCK - LANE]], axis=1) * scale
        ref[...] = jnp.where(y == 0, both[:take], both[skip:skip + take]).T

    def place(half, group, k):
        if k < tiles:
            row, t = (group // 2) * (2 * mid - 2 * (group % 2)) + group % 2, k
        else:
            row, t = mid, group
        lanes = pl.ds(pl.multiple_of((half * tiles + t) * LANE, LANE), LANE)
        out_ref[row * strip:(row + 1) * strip, lanes] = ag[half, group, k]

    pieces = [(group, k) for group in range(4) for k in range(near)]
    for group, k in pieces[:-1]:
        place(c, group, k)
    for group, k in pieces:
        i = near * group + k
        remote(ag.at[1 - c, group, k], ag.at[1 - c, group, k], ac_s.at[i], ac_r.at[i], core_peer).wait_recv()
        if i < len(pieces) - 1:
            place(1 - c, group, k)
    skip = BLOCK // 16 * 8
    folded = jnp.concatenate(
        [ag[0, tiles, tiles].astype(f32)[:skip], ag[1, tiles, tiles].astype(f32)[:BLOCK - skip]], axis=0
    )
    parts = [folded if b == 0 else pltpu.roll(folded, LANE - b * rest, 1) for b in range(in_blocks)]
    out_ref[:, whole:] = jnp.concatenate(parts, axis=0)[:, :rest].astype(bf16)
    for copy in pending:
        copy.wait_send()


def fused(layer_inputs, output_grads, input_inverse, output_inverse):
    tok, in_width = layer_inputs.shape
    out_width = output_grads.shape[1]
    in_blocks, out_blocks = in_width // BLOCK, out_width // BLOCK
    seq = lax.axis_size("seq")
    near = seq // 2
    take = in_width // seq
    step = take // 16 * 16
    window = round_up(BLOCK, 16) - step
    strip = in_width // (near + 1)
    bf16, f32 = jnp.bfloat16, jnp.float32
    vmem = pltpu.VMEM
    dma = pltpu.SemaphoreType.DMA
    g = (strip, LANE)
    f = (2, window, LANE)
    hbm = pl.BlockSpec(memory_space=pltpu.HBM)
    scratch = [
        vmem(layer_inputs.shape, bf16),
        vmem(output_grads.shape, bf16),
        vmem((BLOCK, in_width), f32),
        vmem((BLOCK, out_width), f32),
        dma((4,)),
        vmem((tok, in_blocks * PAD), bf16),
        vmem((tok, out_blocks * PAD), bf16),
        vmem((in_width, tok), bf16),
        vmem((tok, round_up(out_width, LANE)), bf16),
        vmem((4, near, *g), f32),
        vmem((4, near, *g), bf16),
        vmem((4, near, *g), bf16),
        vmem((2, near, *g), bf16),
        vmem((2, near, *g), bf16),
        vmem((near, *g), bf16),
        vmem((near, *g), bf16),
        vmem((near, *g), bf16),
        vmem((near, *g), bf16),
        vmem((seq, *f), f32),
        vmem((seq, *f), bf16),
        vmem((seq, *f), bf16),
        vmem((near, *f), bf16),
        vmem((near, *f), bf16),
        vmem((near, *f), bf16),
        vmem((near, *f), bf16),
        vmem(f, bf16),
        vmem(f, bf16),
        vmem(f, f32),
        vmem(f, f32),
        vmem((2, 4, near, *g), bf16),
    ]
    for count in (5, 2 * near, near, near, near, near, 2, near, 2 * near, 2 * near, 4 * near):
        scratch += [dma((count,)), dma((count,))]
    results = pl.pallas_call(
        functools.partial(kernel, near),
        out_shape=(
            vmem((BLOCK, take), f32),
            vmem((BLOCK, out_width // seq), f32),
            vmem((in_width, out_width), bf16),
        ),
        in_specs=[hbm] * 4,
        out_specs=(pl.BlockSpec(memory_space=vmem),) * 3,
        scratch_shapes=scratch,
        compiler_params=pltpu.CompilerParams(
            collective_id=0, has_side_effects=True, vmem_limit_bytes=62000000
        ),
    )(layer_inputs, output_grads, input_inverse.T, output_inverse.T)
    fx, fy, out = settle(*results)
    return fx.T, fy.T, out


def settle_kernel(a, b, c, a_out, b_out, c_out, sems):
    copies = [
        pltpu.make_async_copy(src, dst, sems.at[i])
        for i, (src, dst) in enumerate(((a, a_out), (b, b_out), (c, c_out)))
    ]
    for copy in copies:
        copy.start()
    for copy in copies:
        copy.wait()


def settle(*arrays):
    return pl.pallas_call(
        settle_kernel,
        out_shape=tuple(jax.ShapeDtypeStruct(a.shape, a.dtype) for a in arrays),
        in_specs=[pl.BlockSpec(memory_space=pltpu.VMEM)] * 3,
        out_specs=(pl.BlockSpec(memory_space=pltpu.HBM),) * 3,
        scratch_shapes=[pltpu.SemaphoreType.DMA((3,))],
        compiler_params=pltpu.CompilerParams(vmem_limit_bytes=4 * 2**20),
    )(*arrays)


def solution(mesh):
    def step(layer_inputs, output_grads, input_inverse, output_inverse):
        in_width, out_width = layer_inputs.shape[1], output_grads.shape[1]
        blocks = in_width // BLOCK
        near = mesh.shape["seq"] // 2
        rest = out_width % LANE
        fits = (
            mesh.shape["batch"] == 4
            and near == 4
            and blocks == near
            and in_width == out_width == blocks * BLOCK
            and out_width // LANE == 2 * (near - 1)
            and in_width % (16 * (near + 1)) == 0
            and rest * blocks == LANE
        )
        body = fused if fits else shards
        return body(layer_inputs, output_grads, input_inverse, output_inverse)

    return jax.shard_map(
        step,
        mesh=mesh,
        in_specs=(P(("batch", "seq"), None), P(("batch", "seq"), None), P(), P()),
        out_specs=(P("seq", None), P("seq", None), P()),
        check_vma=False,
    )
```

time: 46.1 us -> 46.6 us (1.011)
  Pallas kernels: 44.9 us -> 45.8 us
    pallas_call x1, Pallas kernels: 43.7 us -> 44.6 us  [fused(): pl.pallas_call(functools.partial(kernel, near), out_shape=(vmem((BLOCK, t...]
where the time goes in v2:
time: 46.6 us; the launch traced here: 46.4 us
  Pallas kernels  45.8 us (98%)
  between operations  0.64 us (1%)
    pallas_call x1, Pallas kernels, fused(): pl.pallas_call(functools.partial(kernel, near), out_shape=(vmem((BLOCK, t...  44.6 us
    pallas_call x1, Pallas kernels, settle(): pl.pallas_call(settle_kernel, out_shape=tuple((jax.ShapeDtypeStruct(a.sha...  1.19 us

profile of v2, /device:TPU:0, one launch (start us, length us, event | category | flops | bytes accessed | tf_op | source)
XLA Modules:
  0.0 46.4 jit_solution(12170267977178536832)
XLA Ops:
  0.6 44.6 %shard_map.67 = (f32[200,100]{1,0:T(8,128)S(1)}, f32[200,100]{1,0:T(8,128)S(1)}, bf16[800,800]{1,0:T(8,128)(2,1)S(1)}) custom-call(bf16[800,800]{1,0:T(8,128)(2,1)} %x_hbm.1, bf16[800,800]{1,0:T(8,128)(2,1)} %y_hbm.1, f32[200,800]{1,0:T(8,128)} %bitcast.4, f32[200,800]{1,0:T(8,128)} %bitcast.5), custom_call_target="tpu_custom_call" | custom-call | tf_op jit(solution)/shard_map/pallas_call | solution.py:466
  45.2 1.2 %shard_map.68 = (f32[200,100]{1,0:T(8,128)}, f32[200,100]{1,0:T(8,128)}, bf16[800,800]{1,0:T(8,128)(2,1)}) custom-call(f32[200,100]{1,0:T(8,128)S(1)} %get-tuple-element.9.a, f32[200,100]{1,0:T(8,128)S(1)} %get-tuple-element.10.b, bf16[800,800]{1,0:T(8,128)(2,1)S(1)} %get-tuple-element.11.c), custom_call_target="tpu_custom_call" | custom-call | tf_op jit(solution)/shard_map/pallas_call | solution.py:496
